TPU v7x, 128 devices: a whole 4x4x4 slice. The times are simulated.
128 devices in a mesh: obs: 8 (over y, core), src: 16 (over x, z).
Axes of the slice: x: 4, y: 4, z: 4, core: 2. Of those that a mesh axis runs over, the one named last changes fastest.
Arguments:
- data: float32 [1024, 1536], P(('obs', 'src')), may hold values from -170 to 170
- obs_points: float32 [1024, 3, 256], P('obs'), may hold values from 0 to 32, as said below
- src_points: float32 [1024, 3, 256], P('src'), may hold values from -0.4 to 32, as said below
- obs_basis: float32 [1024, 64, 1536], P(('obs', 'src')), may hold values from -0.09375 to 0.09375
- src_basis: float32 [1024, 64, 256], P(('src', 'obs')), may hold values from -0.375 to 0.375
- couplings: float32 [8, 16, 320, 64, 64], P('obs', 'src'), may hold values from -0.75 to 0.75
- near_pairs: int32 [8, 16, 72], P('obs', 'src'), may hold values from -1 to 8191, as said below
- far_pairs: int32 [8, 16, 320], P('obs', 'src'), may hold values from -1 to 8191, as said below
Outputs:
- sources: float32 [1024, 256], P(('src', 'obs'))
- residual: float32 [1024, 1536], P(('obs', 'src'))
- normal_residual: float32 [1024, 256], P(('src', 'obs'))
- misfit: float32 [3], replicated
Inputs may be any that keep to these rules, and one draw needn't show every extreme that they name: Live entries of every block come first and -1 fills the remaining slots; a live entry o * 64 + s pairs local observation leaf o with local source leaf s; no pair is listed twice, and no pair is in both near_pairs and far_pairs. Leaves lie on surface tiles: observation leaf n on tile row (n // 32 + c) % 32, tile column n % 32, with one c of 0 to 3 for all leaves of a draw; source leaf m = j * 64 + h * 8 + l (0 <= h < 8, 0 <= l < 8) on tile row (l % 4) * 8 + h, tile column j * 2 + l // 4. A near pair joins two leaves whose tile rows differ by at most one and whose tile columns differ by at most one. `far_pairs`: live entries of every block come first and -1 fills the remaining slots; a live entry o * 64 + s pairs local observation leaf o with local source leaf s, coupled by the matrix in the same slot of couplings; no pair is listed twice; on the tiles described for near_pairs, the larger of its two leaves' tile row and tile column differences is two or three. `obs_points`: the third coordinate of every observation point lies in [0.5, 0.9]. `src_points`: the third coordinate of every source lies in [-0.4, -0.1].
All inputs are finite; a program needn't handle non-finite values.
Results may differ from a plain program's by a relative error of at most 0.0003.
Values sent between devices are 32-bit elements; how exact they have to be, the bound alone decides.
No kernel may reach another device: no remote copies, remote signals or barrier semaphores. Data moves between devices by JAX's collectives and lax.ppermute only.
A program may use at most 128 MiB of HBM per device.

v0:
```python
import jax
import jax.numpy as jnp
from jax import lax
from jax.sharding import Mesh
from jax.sharding import PartitionSpec as P

ITERS = 2
OBS_SRC = ("obs_0", "obs_1", "src_0", "src_1")
SRC = ("src_0", "src_1")
OBS = ("obs_0", "obs_1")
SRC_OBS = ("src_0", "src_1", "obs_0", "obs_1")
exact = lax.Precision.HIGHEST


def over_axes(value, axes):
    for axis in axes:
        value = lax.psum(value, axis)
    return value


def from_everyone(value, axis):
    copies = jnp.broadcast_to(value, (lax.axis_size(axis), *value.shape))
    return lax.all_to_all(copies, axis, split_axis=0, concat_axis=0, tiled=True)


def laid_out(pieces, dim):
    lengths = list(pieces.shape[1:])
    lengths[dim] *= pieces.shape[0]
    return jnp.moveaxis(pieces, 0, dim).reshape(lengths)


def gathered_copies(value, axis, dim):
    pieces = from_everyone(value, axis)
    return laid_out(pieces, dim)


def side_by_side(arrays, axis, dim, along):
    ends, at = ([], 0)
    for a in arrays[:-1]:
        at += a.shape[along]
        ends.append(at)
    both = jnp.concatenate(arrays, axis=along)
    return tuple(jnp.split(lax.all_gather(both, axis, axis=dim, tiled=True), ends, axis=along))


def cut_along(value, dim, devices):
    before, after = (value.shape[:dim], value.shape[dim + 1 :])
    return jnp.moveaxis(value.reshape(*before, devices, -1, *after), dim, 0)


def summed_on_arrival(value, axis, dim):
    pieces = cut_along(value, dim, lax.axis_size(axis))
    arrived = lax.all_to_all(pieces, axis, split_axis=0, concat_axis=0, tiled=True)
    return arrived.sum(axis=0)


def sent_together(arrays, axis, dim, along):
    widths = [a.shape[along] for a in arrays]
    both = jnp.concatenate(arrays, axis=along)
    out = summed_on_arrival(both, axis, dim)
    return tuple(jnp.split(out, [sum(widths[:k]) for k in range(1, len(widths))], axis=along))


def tensor_parts(obs_pts, src_pts):
    diff_x = obs_pts[:, 0, :, None] - src_pts[:, 0, None, :]
    diff_y = obs_pts[:, 1, :, None] - src_pts[:, 1, None, :]
    diff_z = obs_pts[:, 2, :, None] - src_pts[:, 2, None, :]
    inverse = lax.rsqrt(diff_x * diff_x + diff_y * diff_y + diff_z * diff_z)
    inv_cube = inverse * inverse * inverse / obs_pts.shape[-1]
    inv_fifth = 3.0 * inv_cube * inverse * inverse
    return (
        inv_fifth * diff_x * diff_x - inv_cube,
        inv_fifth * diff_x * diff_y,
        inv_fifth * diff_x * diff_z,
        inv_fifth * diff_y * diff_y - inv_cube,
        inv_fifth * diff_y * diff_z,
        inv_fifth * diff_z * diff_z - inv_cube,
    )


def near_loop(obs_ids, src_ids, pair_count, obs_pts, src_pts, source, target, forward, group_size):
    length = obs_ids.shape[0]
    padding = -length % group_size
    obs_ids = jnp.concatenate([obs_ids, jnp.zeros((padding,), jnp.int32)])
    src_ids = jnp.concatenate([src_ids, jnp.zeros((padding,), jnp.int32)])

    def one_group(group_index, running):
        first_slot = (group_index * group_size).astype(jnp.int32)
        obs_take = lax.dynamic_slice_in_dim(obs_ids, first_slot, group_size)
        src_take = lax.dynamic_slice_in_dim(src_ids, first_slot, group_size)
        in_range = first_slot + jnp.arange(group_size, dtype=jnp.int32) < pair_count
        tensor = tensor_parts(obs_pts[obs_take], src_pts[src_take])
        if forward:
            strengths = jnp.where(in_range[:, None], source[src_take], 0.0)[:, None, :]
            contributions = jnp.stack(
                [jnp.sum(component * strengths, axis=2) for component in tensor], axis=1
            )
            return running.at[obs_take].add(contributions.reshape(group_size, -1))
        residual_rows = jnp.where(in_range[:, None], source[obs_take], 0.0).reshape(
            group_size, 6, -1
        )
        weighted = tensor[0] * residual_rows[:, 0, :, None]
        for which in range(1, 6):
            weighted = weighted + tensor[which] * residual_rows[:, which, :, None]
        return running.at[src_take].add(jnp.sum(weighted, axis=1))

    groups = (pair_count + group_size - 1) // group_size
    return lax.fori_loop(0, groups, one_group, target)


def compact(chosen):
    length = chosen.shape[0]
    position = jnp.cumsum(chosen.astype(jnp.int32)) - 1
    target = jnp.where(chosen, position, length)
    picked = (
        jnp.zeros((length,), jnp.int32)
        .at[target]
        .set(jnp.arange(length, dtype=jnp.int32), mode="drop")
    )
    return (picked, jnp.sum(chosen.astype(jnp.int32)))


def global_total(value):
    return over_axes(value, OBS_SRC)


def paired_totals(first, second):
    return (over_axes(first, OBS_SRC), over_axes(second, OBS_SRC))


def shards(data, obs_points, src_points, obs_basis, src_basis, couplings, near_pairs, far_pairs):
    own_rows = data.shape[0]
    obs_sub = obs_points.shape[0]
    src_sub = src_points.shape[0]
    leaf_size = obs_points.shape[-1]
    rank_size = src_basis.shape[1]
    capacity = near_pairs.shape[-1]
    group_size = 8
    column = lax.axis_index(SRC)
    coupling = couplings[0, 0]
    far_list = far_pairs[0, 0]
    far_live = far_list >= 0
    far_safe = jnp.where(far_live, far_list, 0)
    far_obs = far_safe // src_sub
    far_src = far_safe % src_sub
    row_lists = gathered_copies(near_pairs, SRC, 1)[0].reshape(-1)
    all_points = lax.all_gather(src_points, SRC, axis=0, tiled=True)
    slot_ids = jnp.arange(row_lists.shape[0], dtype=jnp.int32)
    row_safe = jnp.where(row_lists >= 0, row_lists, 0)
    local_obs = row_safe // src_sub
    owned = (row_lists >= 0) & (local_obs // own_rows == column)
    picked, near_count = compact(owned)
    near_obs = jnp.clip(local_obs[picked] - column * own_rows, 0, own_rows - 1)
    near_src = slot_ids[picked] // capacity * src_sub + row_safe[picked] % src_sub
    own_points = lax.dynamic_slice_in_dim(obs_points, column * own_rows, own_rows)

    def far_adjoint(coeff_sub):
        chosen_coeffs = jnp.where(far_live[:, None], coeff_sub[far_obs], 0.0)
        far_terms = jnp.einsum("ckl,ck->cl", coupling, chosen_coeffs, precision=exact)
        return jnp.zeros((src_sub, rank_size), jnp.float32).at[far_src].add(far_terms)

    def apply_adjoint(values):
        coeff_own = jnp.einsum("nkm,nm->nk", obs_basis, values, precision=exact)
        coeff_sub = gathered_copies(coeff_own, SRC, 0)
        near_all = near_loop(
            near_obs,
            near_src,
            near_count,
            own_points,
            all_points,
            values,
            jnp.zeros((all_points.shape[0], leaf_size), jnp.float32),
            False,
            group_size,
        )
        near_block = summed_on_arrival(near_all, SRC, 0)
        coeff_src = far_adjoint(coeff_sub)
        near_own, coeff_back = sent_together((near_block, coeff_src), OBS, 0, 1)
        return near_own + jnp.einsum("nk,nkq->nq", coeff_back, src_basis, precision=exact)

    residual = data
    normal = apply_adjoint(residual)
    gamma_now = global_total(jnp.sum(normal * normal))
    misfit_now = global_total(jnp.sum(residual * residual))
    history = [misfit_now]
    direction = normal
    solution = jnp.zeros_like(normal)
    for iteration in range(ITERS):
        apply_coeff_own = jnp.einsum("nkq,nq->nk", src_basis, direction, precision=exact)
        gathered, apply_coeff_sub = side_by_side((direction, apply_coeff_own), OBS, 0, 1)
        far_chosen_coeffs = jnp.where(far_live[:, None], apply_coeff_sub[far_src], 0.0)
        far_far_terms = jnp.einsum("ckl,cl->ck", coupling, far_chosen_coeffs, precision=exact)
        coeff_obs = jnp.zeros((obs_sub, rank_size), jnp.float32).at[far_obs].add(far_far_terms)
        everything = gathered_copies(gathered, SRC, 0)
        apply_coeff_back = summed_on_arrival(coeff_obs, SRC, 0)
        apply_near_own = near_loop(
            near_obs,
            near_src,
            near_count,
            own_points,
            all_points,
            everything,
            jnp.zeros((own_rows, 6 * leaf_size), jnp.float32),
            True,
            group_size,
        )
        projected = apply_near_own + jnp.einsum(
            "nk,nkm->nm", apply_coeff_back, obs_basis, precision=exact
        )
        curvature, cross_term = paired_totals(
            jnp.sum(projected * projected), jnp.sum(residual * projected)
        )
        step_size = gamma_now / curvature
        solution = solution + step_size * direction
        residual = residual - step_size * projected
        misfit_now = misfit_now - 2.0 * step_size * cross_term + step_size * step_size * curvature
        history.append(misfit_now)
        normal = apply_adjoint(residual)
        gamma_next = global_total(jnp.sum(normal * normal))
        direction = normal + gamma_next / gamma_now * direction
        gamma_now = gamma_next
    return (solution, residual, normal, jnp.stack(history))


def solution(mesh):
    finer = Mesh(mesh.devices.reshape(4, 2, 4, 4), ("obs_0", "obs_1", "src_0", "src_1"))
    return jax.shard_map(
        shards,
        mesh=finer,
        in_specs=(
            P(OBS_SRC, None),
            P(OBS, None, None),
            P(SRC, None, None),
            P(OBS_SRC, None, None),
            P(SRC_OBS, None, None),
            P(OBS, SRC, None, None, None),
            P(OBS, SRC, None),
            P(OBS, SRC, None),
        ),
        out_specs=(P(SRC_OBS, None), P(OBS_SRC, None), P(SRC_OBS, None), P()),
        check_vma=False,
    )
```

profile of v0, /device:TPU:1, one launch (start us, length us, event | category | flops | bytes accessed | tf_op | source)
XLA Modules:
  0.0 791.0 jit_solution(15774144450242854606)
XLA Ops:
  9.4 8.4 %all-to-all-start = ((s32[16,1,1,72]{3,2,1,0:T(1,128)}), s32[16,1,1,72]{3,2,1,0:T(1,128)S(1)}, u32[]{:S(2)}, u32[]{:S(2)}) async-start(s32[16,1,1,72]{3,2,1,0:T(1,128)} %broadcast_in_dim.201), calls=%async_computation | async-start | bytes 16384 | tf_op jit(solution)/shard_map/all_to_all | solution.py:23
  24.2 5.4 all-to-all-start.2
  33.1 6.4 scatter_custom_fusion.5
  39.6 6.5 gather_fusion.16
  46.1 6.5 gather_fusion.17
  52.6 6.5 gather_fusion.15
  60.9 6.0 copy.23
  67.9 45.0 %while.60 = (s32[]{:T(128)}, f32[1024,256]{1,0:T(8,128)}, s32[]{:T(128)}, s32[1152]{0:T(1024)S(1)}, s32[1152]{0:T(1024)S(1)}, /*index=5*/f32[8,3,256]{2,1,0:T(4,...) while((s32[]{:T(128)}, f32[1024,256]{1,0:T(8,128)}, ...), condition=%wide.region_7.8_spmd, body=%wide.region_4.7_spmd.sunk | while | flops 19937348 | bytes 729607 | solution.py:108
  113.0 27.6 %all-to-all-start.1 = ((f32[16,64,256]{2,1,0:T(8,128)}), f32[16,64,256]{2,1,0:T(8,128)}, u32[]{:S(2)}, u32[]{:S(2)}) async-start(f32[16,64,256]{2,1,0:T(8,128)} %bitcast.406), calls=%async_computation.1 | async-start | bytes 2097152 | tf_op jit(solution)/shard_map/all_to_all | solution.py:53
  140.7 12.4 %copy.31 = f32[320,64,64]{2,1,0:T(8,128)} copy(f32[320,64,64]{0,2,1:T(8,128)} %bitcast.404) | data formatting | bytes 10485760 | tf_op jit(solution)/shard_map/squeeze | solution.py:140
  153.1 12.5 %copy.38 = f32[320,64,64]{1,2,0:T(8,128)} copy(f32[320,64,64]{0,2,1:T(8,128)} %bitcast.405) | data formatting | bytes 10485760 | tf_op jit(solution)/shard_map/squeeze | solution.py:140
  168.2 11.5 %fusion.141 = f32[320,1,64]{2,1,0:T(1,128)S(1)} fusion(f32[320,64,1]{1,2,0:T(1,128)S(1)} %bitcast.416, f32[320,64,64]{2,1,0:T(8,128)} %copy.31), kind=kOutput, calls=%fused_computation.424 | convolution fusion | flops 15728640 | bytes 5406720 | tf_op jit(solution)/shard_map/ckl,ck->cl/dot_general | solution.py:159
  184.1 4.3 all-to-all-start.3
  188.4 5.0 all-to-all-done.3
  197.0 13.8 %all_gather.10 = f32[64,320]{1,0:T(8,128)S(1)} all-gather(f32[8,320]{1,0:T(8,128)S(1)} %pad_maximum_fusion), channel_id=1, replica_groups=mesh['obs_0'=4,'obs_1'=2,'src_0'=4,'src_1'=4] {'obs_0','obs_1'}, dimensions={0}, use_global_device_ids=true | all-gather | bytes 92160 | tf_op jit(solution)/shard_map/all_gather | solution.py:43
  212.0 12.2 %fusion.143 = f32[320,1,64]{2,1,0:T(1,128)} fusion(f32[320,64,1]{1,2,0:T(1,128)S(1)} %bitcast.417, f32[320,64,64]{1,2,0:T(8,128)} %copy.38), kind=kOutput, calls=%fused_computation.426 | convolution fusion | flops 15728640 | bytes 5406720 | tf_op jit(solution)/shard_map/ckl,cl->ck/dot_general | solution.py:192
  227.7 6.4 all-to-all-start.5
  234.2 6.5 all-to-all-done.5
  241.7 4.4 all-to-all-start.4
  248.5 12.9 %all-to-all-done.4 = f32[16,64,256]{2,1,0:T(8,128)} async-done(((f32[16,64,256]{2,1,0:T(8,128)}), f32[16,64,256]{2,1,0:T(8,128)}, u32[]{:S(2)}, u32[]{:S(2)}) %all-to-all-start.4) | async-done | bytes 1048608 | tf_op jit(solution)/shard_map/all_to_all | solution.py:23
  261.4 44.4 %while.61 = (s32[]{:T(128)}, f32[8,1536]{1,0:T(8,128)S(1)}, s32[]{:T(128)}, s32[1152]{0:T(1024)S(1)}, f32[8,3,256]{2,1,0:T(4,128)S(1)}, /*index=5*/s32[1152]{0:T...) while((s32[]{:T(128)}, f32[8,1536]{1,0:T(8,128)S(1)}, ...), condition=%wide.region_24.25_spmd, body=%wide.region_16.24_spmd.sunk | while | flops 19927108 | bytes 688647 | solution.py:108
  267.6 4.2 fusion.196
  306.5 18.9 %all-reduce.5 = (f32[]{:T(128)}, f32[]{:T(128)}) all-reduce(f32[]{:T(128)} %get-tuple-element.814, f32[]{:T(128)} %get-tuple-element.694), channel_id=1, replica_groups=mesh['obs_0'=4,'obs_1'=2,'src_0'=4,'src_1'=4] {'obs_0'}, use_global_device_ids=true, to_apply=%region_12.13 | all-reduce | flops 2 | bytes 16 | tf_op jit(solution)/shard_map/psum | solution.py:17
  325.4 17.3 %all-reduce.7 = (f32[]{:T(128)}, f32[]{:T(128)}) all-reduce(f32[]{:T(128)} %get-tuple-element.806, f32[]{:T(128)} %get-tuple-element.807), channel_id=1, replica_groups=mesh['obs_0'=4,'obs_1'=2,'src_0'=4,'src_1'=4] {'obs_1'}, use_global_device_ids=true, to_apply=%region_13.14 | all-reduce | flops 2 | bytes 16 | tf_op jit(solution)/shard_map/psum | solution.py:17
  342.8 6.7 all-reduce.3
  349.5 6.9 all-reduce.1
  366.5 45.4 %while.62 = (s32[]{:T(128)}, f32[1024,256]{1,0:T(8,128)}, s32[]{:T(128)}, s32[1152]{0:T(1024)S(1)}, s32[1152]{0:T(1024)S(1)}, /*index=5*/f32[8,3,256]{2,1,0:T(4,...) while((s32[]{:T(128)}, f32[1024,256]{1,0:T(8,128)}, ...), condition=%wide.region_35.36_spmd, body=%wide.region_32.35_spmd.sunk | while | flops 19937348 | bytes 729607 | solution.py:108
  411.9 29.2 %all-to-all-start.6 = ((f32[16,64,256]{2,1,0:T(8,128)}), f32[16,64,256]{2,1,0:T(8,128)}, u32[]{:S(2)}, u32[]{:S(2)}) async-start(f32[16,64,256]{2,1,0:T(8,128)} %bitcast.407), calls=%async_computation.6 | async-start | bytes 2097152 | tf_op jit(solution)/shard_map/all_to_all | solution.py:53
  443.1 11.5 %fusion.145 = f32[320,1,64]{2,1,0:T(1,128)S(1)} fusion(f32[320,64,1]{1,2,0:T(1,128)S(1)} %bitcast.418, f32[320,64,64]{2,1,0:T(8,128)} %copy.31), kind=kOutput, calls=%fused_computation.428 | convolution fusion | flops 15728640 | bytes 5406720 | tf_op jit(solution)/shard_map/ckl,ck->cl/dot_general | solution.py:159
  458.5 9.7 %all_to_all.70 = f32[8,8,320]{2,1,0:T(8,128)S(1)} all-to-all(f32[8,8,320]{2,1,0:T(8,128)S(1)} %maximum_bitcast_fusion.1), channel_id=1, replica_groups=mesh['obs_0'=4,'obs_1'=2,'src_0'=4,'src_1'=4] {'obs_0','obs_1'}, dimensions={0} | all-to-all | bytes 163840 | tf_op jit(solution)/shard_map/all_to_all | solution.py:53
  470.3 7.5 psum.204
  477.7 5.6 psum.205
  483.3 9.1 %psum.206 = f32[]{:T(128)} all-reduce(f32[]{:T(128)} %psum.205), channel_id=1, replica_groups=mesh['obs_0'=4,'obs_1'=2,'src_0'=4,'src_1'=4] {'src_0'}, use_global_device_ids=true, to_apply=%region_42.43 | all-reduce | flops 1 | bytes 8 | tf_op jit(solution)/shard_map/psum | solution.py:17
  492.4 9.3 %psum.207 = f32[]{:T(128)} all-reduce(f32[]{:T(128)} %psum.206), channel_id=1, replica_groups=mesh['obs_0'=4,'obs_1'=2,'src_0'=4,'src_1'=4] {'src_1'}, use_global_device_ids=true, to_apply=%region_43.44 | all-reduce | flops 1 | bytes 8 | tf_op jit(solution)/shard_map/psum | solution.py:17
  504.6 17.2 %all_gather.11 = f32[64,320]{1,0:T(8,128)S(1)} all-gather(f32[8,320]{1,0:T(8,128)S(1)} %pad_maximum_fusion.1), channel_id=1, replica_groups=mesh['obs_0'=4,'obs_1'=2,'src_0'=4,'src_1'=4] {'obs_0','obs_1'}, dimensions={0}, use_global_device_ids=true | all-gather | bytes 92160 | tf_op jit(solution)/shard_map/all_gather | solution.py:43
  523.8 12.2 %fusion.147 = f32[320,1,64]{2,1,0:T(1,128)} fusion(f32[320,64,1]{1,2,0:T(1,128)S(1)} %bitcast.415, f32[320,64,64]{1,2,0:T(8,128)} %copy.38), kind=kOutput, calls=%fused_computation.430 | convolution fusion | flops 15728640 | bytes 5406720 | tf_op jit(solution)/shard_map/ckl,cl->ck/dot_general | solution.py:192
  543.0 6.4 all-to-all-done.10
  550.4 4.3 all-to-all-start.9
  557.2 13.0 %all-to-all-done.9 = f32[16,64,256]{2,1,0:T(8,128)} async-done(((f32[16,64,256]{2,1,0:T(8,128)}), f32[16,64,256]{2,1,0:T(8,128)}, u32[]{:S(2)}, u32[]{:S(2)}) %all-to-all-start.9) | async-done | bytes 1048608 | tf_op jit(solution)/shard_map/all_to_all | solution.py:23
  570.3 44.4 %while.63 = (s32[]{:T(128)}, f32[8,1536]{1,0:T(8,128)S(1)}, s32[]{:T(128)}, s32[1152]{0:T(1024)S(1)}, f32[8,3,256]{2,1,0:T(4,128)S(1)}, /*index=5*/s32[1152]{0:T...) while((s32[]{:T(128)}, f32[8,1536]{1,0:T(8,128)S(1)}, ...), condition=%wide.region_52.53_spmd, body=%wide.region_44.52_spmd.sunk | while | flops 19927108 | bytes 688647 | solution.py:108
  615.3 18.6 %all-reduce.4 = (f32[]{:T(128)}, f32[]{:T(128)}, f32[]{:T(128)}, f32[]{:T(128)}) all-reduce(f32[]{:T(128)} %get-tuple-element.692, f32[]{:T(128)} %get-tuple-element.695, f32[]{:T(128)} %get-tuple-element.693, f32[]{:T(128)} %get-tuple-element.691), channel_id=1, replica_groups=mesh['obs_0'=4,'obs_1'=2,'src_0'=4,'src_1'=4] {'obs_0'}, use_global_device_ids=true, to_apply=%region_56.57 | all-reduce | flops 4 | bytes 32 | tf_op jit(solution)/shard_map/psum | solution.py:17
  633.9 17.8 %all-reduce.6 = (f32[]{:T(128)}, f32[]{:T(128)}, f32[]{:T(128)}, f32[]{:T(128)}) all-reduce(f32[]{:T(128)} %get-tuple-element.802, f32[]{:T(128)} %get-tuple-element.803, f32[]{:T(128)} %get-tuple-element.804, f32[]{:T(128)} %get-tuple-element.805), channel_id=1, replica_groups=mesh['obs_0'=4,'obs_1'=2,'src_0'=4,'src_1'=4] {'obs_1'}, use_global_device_ids=true, to_apply=%region_57.58 | all-reduce | flops 4 | bytes 32 | tf_op jit(solution)/shard_map/psum | solution.py:17
  651.7 6.7 all-reduce.2
  658.4 6.9 all-reduce
  675.3 45.0 %while.64 = (s32[]{:T(128)}, f32[1024,256]{1,0:T(8,128)}, s32[]{:T(128)}, s32[1152]{0:T(1024)S(1)}, s32[1152]{0:T(1024)S(1)}, /*index=5*/f32[8,3,256]{2,1,0:T(4,...) while((s32[]{:T(128)}, f32[1024,256]{1,0:T(8,128)}, ...), condition=%wide.region_63.64_spmd, body=%wide.region_60.63_spmd.sunk | while | flops 19937348 | bytes 729607 | solution.py:108
  720.4 29.0 %all-to-all-start.11 = ((f32[16,64,256]{2,1,0:T(8,128)}), f32[16,64,256]{2,1,0:T(8,128)}, u32[]{:S(2)}, u32[]{:S(2)}) async-start(f32[16,64,256]{2,1,0:T(8,128)} %bitcast.408), calls=%async_computation.11 | async-start | bytes 2097152 | tf_op jit(solution)/shard_map/all_to_all | solution.py:53
  755.1 11.5 %fusion.149 = f32[320,1,64]{2,1,0:T(1,128)S(1)} fusion(f32[320,64,1]{1,2,0:T(1,128)S(1)} %bitcast.414, f32[320,64,64]{2,1,0:T(8,128)} %copy.31), kind=kOutput, calls=%fused_computation.432 | convolution fusion | flops 15728640 | bytes 5406720 | tf_op jit(solution)/shard_map/ckl,ck->cl/dot_general | solution.py:159
  771.1 5.6 all-to-all-start.13
  (573 shorter events, 305.4 us)
Async XLA Ops:
  7.2 10.6 %copy-start = (f32[8,64,1536]{2,1,0:T(8,128)S(1)}, f32[8,64,1536]{2,1,0:T(8,128)}, u32[]{:S(2)}) copy-start(f32[8,64,1536]{2,1,0:T(8,128)} %param.21) | copy-start | bytes 9437188
  7.2 53.7 %all-gather.2.cloned.1.call-start = ((), (), s32[]{:S(2)}) async-start(), calls=%async_computation.14 | async-start | bytes 3342336 | tf_op jit(solution)/shard_map/all_gather | solution.py:147
  9.4 14.8 %all-to-all-start = ((s32[16,1,1,72]{3,2,1,0:T(1,128)}), s32[16,1,1,72]{3,2,1,0:T(1,128)S(1)}, u32[]{:S(2)}, u32[]{:S(2)}) async-start(s32[16,1,1,72]{3,2,1,0:T(1,128)} %broadcast_in_dim.201), calls=%async_computation | async-start | bytes 16384 | tf_op jit(solution)/shard_map/all_to_all | solution.py:23
  24.2 88.8 %all-to-all-start.2 = ((f32[16,1,512]{2,1,0:T(1,128)}), f32[16,1,512]{2,1,0:T(1,128)S(1)}, u32[]{:S(2)}, u32[]{:S(2)}) async-start(f32[16,1,512]{2,1,0:T(1,128)} %reshape.846), calls=%async_computation.2 | async-start | bytes 65536 | tf_op jit(solution)/shard_map/all_to_all | solution.py:23
  59.1 8.8 %copy-start.1 = (f32[8,1536]{1,0:T(8,128)S(1)}, f32[8,1536]{1,0:T(8,128)}, u32[]{:S(2)}) copy-start(f32[8,1536]{1,0:T(8,128)} %param.18) | copy-start | bytes 147460
  113.0 40.1 %copy-start.3 = (s32[1152]{0:T(1024)}, s32[1152]{0:T(1024)S(1)}, u32[]{:S(2)}) copy-start(s32[1152]{0:T(1024)S(1)} %get-tuple-element.1530) | copy-start | bytes 13828
  113.0 27.6 %copy-start.16 = (s32[1,1,320]{2,1,0:T(1,128)S(1)}, s32[1,1,320]{2,1,0:T(1,128)}, u32[]{:S(2)}) copy-start(s32[1,1,320]{2,1,0:T(1,128)} %param.25) | copy-start | bytes 3844
  113.0 69.2 %all-to-all-start.1 = ((f32[16,64,256]{2,1,0:T(8,128)}), f32[16,64,256]{2,1,0:T(8,128)}, u32[]{:S(2)}, u32[]{:S(2)}) async-start(f32[16,64,256]{2,1,0:T(8,128)} %bitcast.406), calls=%async_computation.1 | async-start | bytes 2097152 | tf_op jit(solution)/shard_map/all_to_all | solution.py:53
  140.6 47.8 %copy-start.14 = (s32[320]{0:T(512)}, s32[320]{0:T(512)S(1)}, u32[]{:S(2)}) copy-start(s32[320]{0:T(512)S(1)} %get-tuple-element.699) | copy-start | bytes 3844
  140.7 83.5 %copy-start.15 = (s32[320]{0:T(512)}, s32[320]{0:T(512)S(1)}, u32[]{:S(2)}) copy-start(s32[320]{0:T(512)S(1)} %get-tuple-element.698) | copy-start | bytes 3844
  165.6 14.1 %copy-start.7 = (s32[1024]{0:T(1024)}, s32[1024]{0:T(1024)S(1)}, u32[]{:S(2)}) copy-start(s32[1024]{0:T(1024)S(1)} %pad_clamp_fusion.12) | copy-start | bytes 12292
  165.7 46.2 %copy-start.10 = (pred[320]{0:T(512)(128)(4,1)}, pred[320]{0:T(512)(128)(4,1)S(1)}, u32[]{:S(2)}) copy-start(pred[320]{0:T(512)(128)(4,1)S(1)} %compare_reduce_fusion) | copy-start | bytes 964
  184.1 9.3 %all-to-all-start.3 = ((f32[8,8,320]{2,1,0:T(8,128)}), f32[8,8,320]{2,1,0:T(8,128)S(1)}, u32[]{:S(2)}, u32[]{:S(2)}) async-start(f32[8,8,320]{2,1,0:T(8,128)} %maximum_bitcast_fusion), calls=%async_computation.3 | async-start | bytes 196608 | tf_op jit(solution)/shard_map/all_to_all | solution.py:53
  188.4 35.8 %copy-start.13 = (s32[1024]{0:T(1024)}, s32[1024]{0:T(1024)S(1)}, u32[]{:S(2)}) copy-start(s32[1024]{0:T(1024)S(1)} %pad_clamp_fusion.11) | copy-start | bytes 12292
  227.7 12.9 %all-to-all-start.5 = ((f32[16,1,512]{2,1,0:T(1,128)}), f32[16,1,512]{2,1,0:T(1,128)S(1)}, u32[]{:S(2)}, u32[]{:S(2)}) async-start(f32[16,1,512]{2,1,0:T(1,128)} %reshape.848), calls=%async_computation.5 | async-start | bytes 65536 | tf_op jit(solution)/shard_map/all_to_all | solution.py:53
  241.7 19.7 %all-to-all-start.4 = ((f32[16,64,256]{2,1,0:T(8,128)}), f32[16,64,256]{2,1,0:T(8,128)}, u32[]{:S(2)}, u32[]{:S(2)}) async-start(f32[16,64,256]{2,1,0:T(8,128)} %broadcast_in_dim.208), calls=%async_computation.4 | async-start | bytes 2097152 | tf_op jit(solution)/shard_map/all_to_all | solution.py:23
  246.0 15.4 %copy-start.4 = (s32[1152]{0:T(1024)S(1)}, s32[1152]{0:T(1024)}, u32[]{:S(2)}) copy-start(s32[1152]{0:T(1024)} %copy-done.3) | copy-start | bytes 13828
  361.1 50.8 %all-to-all-start.7 = ((f32[16,1,512]{2,1,0:T(1,128)}), f32[16,1,512]{2,1,0:T(1,128)S(1)}, u32[]{:S(2)}, u32[]{:S(2)}) async-start(f32[16,1,512]{2,1,0:T(1,128)} %reshape.850), calls=%async_computation.7 | async-start | bytes 65536 | tf_op jit(solution)/shard_map/all_to_all | solution.py:23
  411.9 42.7 %copy-start.5 = (s32[1152]{0:T(1024)}, s32[1152]{0:T(1024)S(1)}, u32[]{:S(2)}) copy-start(s32[1152]{0:T(1024)S(1)} %get-tuple-element.1532) | copy-start | bytes 13828
  411.9 30.0 %copy-start.8 = (s32[1024]{0:T(1024)S(1)}, s32[1024]{0:T(1024)}, u32[]{:S(2)}) copy-start(s32[1024]{0:T(1024)} %copy-done.7) | copy-start | bytes 12292
  411.9 31.1 %copy-start.11 = (pred[320]{0:T(512)(128)(4,1)S(1)}, pred[320]{0:T(512)(128)(4,1)}, u32[]{:S(2)}) copy-start(pred[320]{0:T(512)(128)(4,1)} %copy-done.10) | copy-start | bytes 964
  411.9 45.3 %all-to-all-start.6 = ((f32[16,64,256]{2,1,0:T(8,128)}), f32[16,64,256]{2,1,0:T(8,128)}, u32[]{:S(2)}, u32[]{:S(2)}) async-start(f32[16,64,256]{2,1,0:T(8,128)} %bitcast.407), calls=%async_computation.6 | async-start | bytes 2097152 | tf_op jit(solution)/shard_map/all_to_all | solution.py:53
  539.5 9.9 %all-to-all-start.10 = ((f32[16,1,512]{2,1,0:T(1,128)}), f32[16,1,512]{2,1,0:T(1,128)S(1)}, u32[]{:S(2)}, u32[]{:S(2)}) async-start(f32[16,1,512]{2,1,0:T(1,128)} %reshape.852), calls=%async_computation.10 | async-start | bytes 65536 | tf_op jit(solution)/shard_map/all_to_all | solution.py:53
  550.4 19.8 %all-to-all-start.9 = ((f32[16,64,256]{2,1,0:T(8,128)}), f32[16,64,256]{2,1,0:T(8,128)}, u32[]{:S(2)}, u32[]{:S(2)}) async-start(f32[16,64,256]{2,1,0:T(8,128)} %broadcast_in_dim.210), calls=%async_computation.9 | async-start | bytes 2097152 | tf_op jit(solution)/shard_map/all_to_all | solution.py:23
  554.8 15.5 %copy-start.6 = (s32[1152]{0:T(1024)S(1)}, s32[1152]{0:T(1024)}, u32[]{:S(2)}) copy-start(s32[1152]{0:T(1024)} %copy-done.5) | copy-start | bytes 13828
  670.1 50.3 %all-to-all-start.12 = ((f32[16,1,512]{2,1,0:T(1,128)}), f32[16,1,512]{2,1,0:T(1,128)S(1)}, u32[]{:S(2)}, u32[]{:S(2)}) async-start(f32[16,1,512]{2,1,0:T(1,128)} %reshape.854), calls=%async_computation.12 | async-start | bytes 65536 | tf_op jit(solution)/shard_map/all_to_all | solution.py:23
  720.4 46.2 %copy-start.2 = (f32[8,1536]{1,0:T(8,128)}, f32[8,1536]{1,0:T(8,128)S(1)}, u32[]{:S(2)}) copy-start(f32[8,1536]{1,0:T(8,128)S(1)} %get-tuple-element.1496) | copy-start | bytes 147460
  720.4 33.5 %copy-start.9 = (s32[1024]{0:T(1024)S(1)}, s32[1024]{0:T(1024)}, u32[]{:S(2)}) copy-start(s32[1024]{0:T(1024)} %copy-done.7) | copy-start | bytes 12292
  720.4 34.6 %copy-start.12 = (pred[320]{0:T(512)(128)(4,1)S(1)}, pred[320]{0:T(512)(128)(4,1)}, u32[]{:S(2)}) copy-start(pred[320]{0:T(512)(128)(4,1)} %copy-done.10) | copy-start | bytes 964
  720.4 48.8 %all-to-all-start.11 = ((f32[16,64,256]{2,1,0:T(8,128)}), f32[16,64,256]{2,1,0:T(8,128)}, u32[]{:S(2)}, u32[]{:S(2)}) async-start(f32[16,64,256]{2,1,0:T(8,128)} %bitcast.408), calls=%async_computation.11 | async-start | bytes 2097152 | tf_op jit(solution)/shard_map/all_to_all | solution.py:53
  771.1 10.6 %all-to-all-start.13 = ((f32[8,8,320]{2,1,0:T(8,128)}), f32[8,8,320]{2,1,0:T(8,128)S(1)}, u32[]{:S(2)}, u32[]{:S(2)}) async-start(f32[8,8,320]{2,1,0:T(8,128)} %maximum_bitcast_fusion.2), calls=%async_computation.13 | async-start | bytes 196608 | tf_op jit(solution)/shard_map/all_to_all | solution.py:53
Sparse Core Ops, SparseCore 0:
  10.2 50.6 all-gather.1
where the time goes:
time: 803 us; the launch traced here: 791 us
  blocking collectives  172 us (21%)
  local copies, waits for them, and re-layouts  165 us (21%)
  other arithmetic  163 us (20%)
  starting transfers between devices  136 us (17%)
  matrix products  78.4 us (10%)
  waiting for transfers between devices  51.3 us (6%)
  between operations  22.9 us (3%)
    psum x12, blocking collectives, over_axes(): value = lax.psum(value, axis)  131 us
    all_to_all x7, starting transfers between devices, summed_on_arrival(): lax.all_to_all(pieces, axis, split_axis=0, concat_axis=0, tiled=True)  106 us
    gather x40, local copies, waits for them, and re-layouts, one_group(): tensor = tensor_parts(obs_pts[obs_take], src_pts[src_take])  66.8 us
    reduce_sum x12, other arithmetic, one_group(): return running.at[src_take].add(jnp.sum(weighted, axis=1))  42.9 us
    dot_general x3, matrix products, far_adjoint(): jnp.einsum('ckl,ck->cl', coupling, chosen_coeffs, precision=exact)  34.6 us
    scatter-add x12, other arithmetic, one_group(): return running.at[src_take].add(jnp.sum(weighted, axis=1))  33.8 us
    reduce_sum x8, other arithmetic, one_group(): jnp.sum(component * strengths, axis=2)  33.7 us
    all_gather x2, blocking collectives, side_by_side(): lax.all_gather(both, axis, axis=dim, tiled=True)  31 us
  transfers between devices with their start and end apart: 14, of which 8 were waited for; matrix products, arithmetic and copies ran while one was open for 33% of the time, Pallas kernels for 0%

commit v1 on v0

--- a/solution.py
+++ b/solution.py
@@ -14,7 +14,7 @@
 
 def over_axes(value, axes):
     for axis in axes:
-        value = lax.psum(value, axis)
+        value = jnp.sum(lax.all_gather(value, axis), axis=0)
     return value
 
 

time: 803 us -> 848 us (1.056)
  local copies, waits for them, and re-layouts: 165 us -> 206 us
  other arithmetic: 163 us -> 179 us
  blocking collectives: 172 us -> 163 us
    psum x12 -> x0, blocking collectives: 131 us -> none  [over_axes(): value = lax.psum(value, axis)]
    unnamed x0 -> x12, blocking collectives: none -> 123 us
    unnamed x45 -> x113, local copies, waits for them, and re-layouts: 4.07 us -> 45.6 us
    reduce_sum x0 -> x28, other arithmetic: none -> 16.9 us  [over_axes(): value = jnp.sum(lax.all_gather(value, axis), axis=0)]
  transfers between devices with their start and end apart: 14 -> 14, of which waited for: 8 -> 8; matrix products, arithmetic and copies ran while one was open for 33% -> 32% of each run, Pallas kernels for 0% -> 0%
where the time goes in v1:
time: 848 us; the launch traced here: 836 us
  local copies, waits for them, and re-layouts  206 us (24%)
  other arithmetic  179 us (21%)
  blocking collectives  163 us (19%)
  starting transfers between devices  137 us (16%)
  matrix products  78.4 us (9%)
  waiting for transfers between devices  46.8 us (6%)
  between operations  22.7 us (3%)
    unnamed x12, blocking collectives  123 us
    all_to_all x7, starting transfers between devices, summed_on_arrival(): lax.all_to_all(pieces, axis, split_axis=0, concat_axis=0, tiled=True)  106 us
    gather x40, local copies, waits for them, and re-layouts, one_group(): tensor = tensor_parts(obs_pts[obs_take], src_pts[src_take])  66.8 us
    unnamed x113, local copies, waits for them, and re-layouts  45.6 us
    reduce_sum x12, other arithmetic, one_group(): return running.at[src_take].add(jnp.sum(weighted, axis=1))  42.9 us
    dot_general x3, matrix products, far_adjoint(): jnp.einsum('ckl,ck->cl', coupling, chosen_coeffs, precision=exact)  34.6 us
    reduce_sum x8, other arithmetic, one_group(): jnp.sum(component * strengths, axis=2)  33.7 us
    scatter-add x12, other arithmetic, one_group(): return running.at[src_take].add(jnp.sum(weighted, axis=1))  33.4 us
  transfers between devices with their start and end apart: 14, of which 8 were waited for; matrix products, arithmetic and copies ran while one was open for 32% of the time, Pallas kernels for 0%

profile of v1, /device:TPU:1, one launch (start us, length us, event | category | flops | bytes accessed | tf_op | source)
XLA Modules:
  0.0 835.9 jit_solution(41711639222879449)
XLA Ops:
  9.4 8.4 %all-to-all-start = ((s32[16,1,1,72]{3,2,1,0:T(1,128)}), s32[16,1,1,72]{3,2,1,0:T(1,128)S(1)}, u32[]{:S(2)}, u32[]{:S(2)}) async-start(s32[16,1,1,72]{3,2,1,0:T(1,128)} %broadcast_in_dim.201), calls=%async_computation | async-start | bytes 16384 | tf_op jit(solution)/shard_map/all_to_all | solution.py:23
  24.2 5.4 all-to-all-start.2
  33.1 6.4 scatter_custom_fusion.5
  39.6 6.5 gather_fusion.16
  46.1 6.5 gather_fusion.17
  52.6 6.5 gather_fusion.15
  60.9 6.0 copy.23
  67.9 45.0 %while.60 = (s32[]{:T(128)}, f32[1024,256]{1,0:T(8,128)}, s32[]{:T(128)}, s32[1152]{0:T(1024)S(1)}, s32[1152]{0:T(1024)S(1)}, /*index=5*/f32[8,3,256]{2,1,0:T(4,...) while((s32[]{:T(128)}, f32[1024,256]{1,0:T(8,128)}, ...), condition=%wide.region_7.8_spmd, body=%wide.region_4.7_spmd.sunk | while | flops 19937348 | bytes 729607 | solution.py:108
  113.0 27.9 %all-to-all-start.1 = ((f32[16,64,256]{2,1,0:T(8,128)}), f32[16,64,256]{2,1,0:T(8,128)}, u32[]{:S(2)}, u32[]{:S(2)}) async-start(f32[16,64,256]{2,1,0:T(8,128)} %bitcast.438), calls=%async_computation.1 | async-start | bytes 2097152 | tf_op jit(solution)/shard_map/all_to_all | solution.py:53
  140.9 12.4 %copy.31 = f32[320,64,64]{2,1,0:T(8,128)} copy(f32[320,64,64]{0,2,1:T(8,128)} %bitcast.436) | data formatting | bytes 10485760 | tf_op jit(solution)/shard_map/squeeze | solution.py:140
  153.3 12.5 %copy.38 = f32[320,64,64]{1,2,0:T(8,128)} copy(f32[320,64,64]{0,2,1:T(8,128)} %bitcast.437) | data formatting | bytes 10485760 | tf_op jit(solution)/shard_map/squeeze | solution.py:140
  168.4 11.5 %fusion.141 = f32[320,1,64]{2,1,0:T(1,128)S(1)} fusion(f32[320,64,1]{1,2,0:T(1,128)S(1)} %bitcast.448, f32[320,64,64]{2,1,0:T(8,128)} %copy.31), kind=kOutput, calls=%fused_computation.424 | convolution fusion | flops 15728640 | bytes 5406720 | tf_op jit(solution)/shard_map/ckl,ck->cl/dot_general | solution.py:159
  184.4 4.3 all-to-all-start.3
  188.7 5.0 all-to-all-done.3
  197.3 13.6 %all_gather.186 = f32[64,320]{1,0:T(8,128)S(1)} all-gather(f32[8,320]{1,0:T(8,128)S(1)} %pad_maximum_fusion), channel_id=1, replica_groups=mesh['obs_0'=4,'obs_1'=2,'src_0'=4,'src_1'=4] {'obs_0','obs_1'}, dimensions={0}, use_global_device_ids=true | all-gather | bytes 92160 | tf_op jit(solution)/shard_map/all_gather | solution.py:43
  212.0 12.2 %fusion.143 = f32[320,1,64]{2,1,0:T(1,128)} fusion(f32[320,64,1]{1,2,0:T(1,128)S(1)} %bitcast.449, f32[320,64,64]{1,2,0:T(8,128)} %copy.38), kind=kOutput, calls=%fused_computation.426 | convolution fusion | flops 15728640 | bytes 5406720 | tf_op jit(solution)/shard_map/ckl,cl->ck/dot_general | solution.py:192
  227.7 6.4 all-to-all-start.5
  234.2 6.5 all-to-all-done.5
  241.7 4.4 all-to-all-start.4
  250.4 11.0 %all-to-all-done.4 = f32[16,64,256]{2,1,0:T(8,128)} async-done(((f32[16,64,256]{2,1,0:T(8,128)}), f32[16,64,256]{2,1,0:T(8,128)}, u32[]{:S(2)}, u32[]{:S(2)}) %all-to-all-start.4) | async-done | bytes 1048608 | tf_op jit(solution)/shard_map/all_to_all | solution.py:23
  261.5 44.4 %while.61 = (s32[]{:T(128)}, f32[8,1536]{1,0:T(8,128)S(1)}, s32[]{:T(128)}, s32[1152]{0:T(1024)S(1)}, f32[8,3,256]{2,1,0:T(4,128)S(1)}, /*index=5*/s32[1152]{0:T...) while((s32[]{:T(128)}, f32[8,1536]{1,0:T(8,128)S(1)}, ...), condition=%wide.region_24.25_spmd, body=%wide.region_16.24_spmd.sunk | while | flops 19927108 | bytes 688647 | solution.py:108
  308.6 18.3 %all-reduce.33 = (f32[4]{0:T(128)S(1)}, f32[4]{0:T(128)S(1)}) all-reduce(f32[4]{0:T(128)S(1)} %dynamic-update-slice, f32[4]{0:T(128)S(1)} %dynamic-update-slice.4), channel_id=1, replica_groups=mesh['obs_0'=4,'obs_1'=2,'src_0'=4,'src_1'=4] {'obs_0'}, use_global_device_ids=true, to_apply=%add | all-reduce | flops 8 | bytes 64
  331.4 16.7 %all-reduce.35 = (f32[2]{0:T(128)S(1)}, f32[2]{0:T(128)S(1)}) all-reduce(f32[2]{0:T(128)S(1)} %dynamic-update-slice.1, f32[2]{0:T(128)S(1)} %dynamic-update-slice.5), channel_id=1, replica_groups=mesh['obs_0'=4,'obs_1'=2,'src_0'=4,'src_1'=4] {'obs_1'}, use_global_device_ids=true, to_apply=%add.1 | all-reduce | flops 4 | bytes 32
  353.2 6.1 all-reduce.31
  363.2 6.0 all-reduce.29
  380.2 45.0 %while.62 = (s32[]{:T(128)}, f32[1024,256]{1,0:T(8,128)}, s32[]{:T(128)}, s32[1152]{0:T(1024)S(1)}, s32[1152]{0:T(1024)S(1)}, /*index=5*/f32[8,3,256]{2,1,0:T(4,...) while((s32[]{:T(128)}, f32[1024,256]{1,0:T(8,128)}, ...), condition=%wide.region_35.36_spmd, body=%wide.region_32.35_spmd.sunk | while | flops 19937348 | bytes 729607 | solution.py:108
  425.3 29.0 %all-to-all-start.6 = ((f32[16,64,256]{2,1,0:T(8,128)}), f32[16,64,256]{2,1,0:T(8,128)}, u32[]{:S(2)}, u32[]{:S(2)}) async-start(f32[16,64,256]{2,1,0:T(8,128)} %bitcast.439), calls=%async_computation.6 | async-start | bytes 2097152 | tf_op jit(solution)/shard_map/all_to_all | solution.py:53
  456.2 11.5 %fusion.145 = f32[320,1,64]{2,1,0:T(1,128)S(1)} fusion(f32[320,64,1]{1,2,0:T(1,128)S(1)} %bitcast.450, f32[320,64,64]{2,1,0:T(8,128)} %copy.31), kind=kOutput, calls=%fused_computation.428 | convolution fusion | flops 15728640 | bytes 5406720 | tf_op jit(solution)/shard_map/ckl,ck->cl/dot_general | solution.py:159
  471.7 9.7 %all_to_all.70 = f32[8,8,320]{2,1,0:T(8,128)S(1)} all-to-all(f32[8,8,320]{2,1,0:T(8,128)S(1)} %maximum_bitcast_fusion.1), channel_id=1, replica_groups=mesh['obs_0'=4,'obs_1'=2,'src_0'=4,'src_1'=4] {'obs_0','obs_1'}, dimensions={0} | all-to-all | bytes 163840 | tf_op jit(solution)/shard_map/all_to_all | solution.py:53
  484.8 6.8 all-reduce.8
  493.6 4.9 all-reduce.9
  500.6 8.7 %all-reduce.10 = f32[4]{0:T(128)S(1)} all-reduce(f32[4]{0:T(128)S(1)} %dynamic-update-slice.10), channel_id=1, replica_groups=mesh['obs_0'=4,'obs_1'=2,'src_0'=4,'src_1'=4] {'src_0'}, use_global_device_ids=true, to_apply=%add.10 | all-reduce | flops 4 | bytes 32
  511.2 8.6 %all-reduce.11 = f32[4]{0:T(128)S(1)} all-reduce(f32[4]{0:T(128)S(1)} %dynamic-update-slice.11), channel_id=1, replica_groups=mesh['obs_0'=4,'obs_1'=2,'src_0'=4,'src_1'=4] {'src_1'}, use_global_device_ids=true, to_apply=%add.11 | all-reduce | flops 4 | bytes 32
  523.3 17.0 %all_gather.203 = f32[64,320]{1,0:T(8,128)S(1)} all-gather(f32[8,320]{1,0:T(8,128)S(1)} %pad_maximum_fusion.1), channel_id=1, replica_groups=mesh['obs_0'=4,'obs_1'=2,'src_0'=4,'src_1'=4] {'obs_0','obs_1'}, dimensions={0}, use_global_device_ids=true | all-gather | bytes 92160 | tf_op jit(solution)/shard_map/all_gather | solution.py:43
  542.2 12.2 %fusion.147 = f32[320,1,64]{2,1,0:T(1,128)} fusion(f32[320,64,1]{1,2,0:T(1,128)S(1)} %bitcast.447, f32[320,64,64]{1,2,0:T(8,128)} %copy.38), kind=kOutput, calls=%fused_computation.430 | convolution fusion | flops 15728640 | bytes 5406720 | tf_op jit(solution)/shard_map/ckl,cl->ck/dot_general | solution.py:192
  561.4 6.4 all-to-all-done.10
  568.8 4.3 all-to-all-start.9
  578.3 10.4 %all-to-all-done.9 = f32[16,64,256]{2,1,0:T(8,128)} async-done(((f32[16,64,256]{2,1,0:T(8,128)}), f32[16,64,256]{2,1,0:T(8,128)}, u32[]{:S(2)}, u32[]{:S(2)}) %all-to-all-start.9) | async-done | bytes 1048608 | tf_op jit(solution)/shard_map/all_to_all | solution.py:23
  588.7 44.4 %while.63 = (s32[]{:T(128)}, f32[8,1536]{1,0:T(8,128)S(1)}, s32[]{:T(128)}, s32[1152]{0:T(1024)S(1)}, f32[8,3,256]{2,1,0:T(4,128)S(1)}, /*index=5*/s32[1152]{0:T...) while((s32[]{:T(128)}, f32[8,1536]{1,0:T(8,128)S(1)}, ...), condition=%wide.region_52.53_spmd, body=%wide.region_44.52_spmd.sunk | while | flops 19927108 | bytes 688647 | solution.py:108
  605.9 4.2 fusion.202
  636.7 17.9 %all-reduce.32 = (f32[4]{0:T(128)S(1)}, f32[4]{0:T(128)S(1)}, f32[4]{0:T(128)S(1)}, f32[4]{0:T(128)S(1)}) all-reduce(f32[4]{0:T(128)S(1)} %dynamic-update-slice.12, f32[4]{0:T(128)S(1)} %dynamic-update-slice.16, f32[4]{0:T(128)S(1)} %dynamic-update-slice.20, ...), channel_id=1, replica_groups=mesh['obs_0'=4,'obs_1'=2,'src_0'=4,'src_1'=4] {'obs_0'}, use_global_device_ids=true, to_apply=%add.12 | all-reduce | flops 16 | bytes 128
  662.4 17.1 %all-reduce.34 = (f32[2]{0:T(128)S(1)}, f32[2]{0:T(128)S(1)}, f32[2]{0:T(128)S(1)}, f32[2]{0:T(128)S(1)}) all-reduce(f32[2]{0:T(128)S(1)} %dynamic-update-slice.13, f32[2]{0:T(128)S(1)} %dynamic-update-slice.17, f32[2]{0:T(128)S(1)} %dynamic-update-slice.21, ...), channel_id=1, replica_groups=mesh['obs_0'=4,'obs_1'=2,'src_0'=4,'src_1'=4] {'obs_1'}, use_global_device_ids=true, to_apply=%add.13 | all-reduce | flops 8 | bytes 64
  687.7 6.1 all-reduce.30
  701.6 6.0 all-reduce.28
  718.2 45.0 %while.64 = (s32[]{:T(128)}, f32[1024,256]{1,0:T(8,128)}, s32[]{:T(128)}, s32[1152]{0:T(1024)S(1)}, s32[1152]{0:T(1024)S(1)}, /*index=5*/f32[8,3,256]{2,1,0:T(4,...) while((s32[]{:T(128)}, f32[1024,256]{1,0:T(8,128)}, ...), condition=%wide.region_63.64_spmd, body=%wide.region_60.63_spmd.sunk | while | flops 19937348 | bytes 729607 | solution.py:108
  763.3 29.2 %all-to-all-start.11 = ((f32[16,64,256]{2,1,0:T(8,128)}), f32[16,64,256]{2,1,0:T(8,128)}, u32[]{:S(2)}, u32[]{:S(2)}) async-start(f32[16,64,256]{2,1,0:T(8,128)} %bitcast.440), calls=%async_computation.11 | async-start | bytes 2097152 | tf_op jit(solution)/shard_map/all_to_all | solution.py:53
  800.1 11.5 %fusion.149 = f32[320,1,64]{2,1,0:T(1,128)S(1)} fusion(f32[320,64,1]{1,2,0:T(1,128)S(1)} %bitcast.446, f32[320,64,64]{2,1,0:T(8,128)} %copy.31), kind=kOutput, calls=%fused_computation.432 | convolution fusion | flops 15728640 | bytes 5406720 | tf_op jit(solution)/shard_map/ckl,ck->cl/dot_general | solution.py:159
  816.2 5.6 all-to-all-start.13
  (669 shorter events, 363.3 us)
Async XLA Ops:
  7.2 10.6 %copy-start = (f32[8,64,1536]{2,1,0:T(8,128)S(1)}, f32[8,64,1536]{2,1,0:T(8,128)}, u32[]{:S(2)}) copy-start(f32[8,64,1536]{2,1,0:T(8,128)} %param.21) | copy-start | bytes 9437188
  7.2 53.7 %all-gather.2.cloned.1.call-start = ((), (), s32[]{:S(2)}) async-start(), calls=%async_computation.14 | async-start | bytes 3342336 | tf_op jit(solution)/shard_map/all_gather | solution.py:147
  9.4 14.8 %all-to-all-start = ((s32[16,1,1,72]{3,2,1,0:T(1,128)}), s32[16,1,1,72]{3,2,1,0:T(1,128)S(1)}, u32[]{:S(2)}, u32[]{:S(2)}) async-start(s32[16,1,1,72]{3,2,1,0:T(1,128)} %broadcast_in_dim.201), calls=%async_computation | async-start | bytes 16384 | tf_op jit(solution)/shard_map/all_to_all | solution.py:23
  24.2 88.8 %all-to-all-start.2 = ((f32[16,1,512]{2,1,0:T(1,128)}), f32[16,1,512]{2,1,0:T(1,128)S(1)}, u32[]{:S(2)}, u32[]{:S(2)}) async-start(f32[16,1,512]{2,1,0:T(1,128)} %reshape.986), calls=%async_computation.2 | async-start | bytes 65536 | tf_op jit(solution)/shard_map/all_to_all | solution.py:23
  59.1 8.8 %copy-start.1 = (f32[8,1536]{1,0:T(8,128)S(1)}, f32[8,1536]{1,0:T(8,128)}, u32[]{:S(2)}) copy-start(f32[8,1536]{1,0:T(8,128)} %param.18) | copy-start | bytes 147460
  113.0 40.4 %copy-start.3 = (s32[1152]{0:T(1024)}, s32[1152]{0:T(1024)S(1)}, u32[]{:S(2)}) copy-start(s32[1152]{0:T(1024)S(1)} %get-tuple-element.1530) | copy-start | bytes 13828
  113.0 27.9 %copy-start.16 = (s32[1,1,320]{2,1,0:T(1,128)S(1)}, s32[1,1,320]{2,1,0:T(1,128)}, u32[]{:S(2)}) copy-start(s32[1,1,320]{2,1,0:T(1,128)} %param.25) | copy-start | bytes 3844
  113.0 69.4 %all-to-all-start.1 = ((f32[16,64,256]{2,1,0:T(8,128)}), f32[16,64,256]{2,1,0:T(8,128)}, u32[]{:S(2)}, u32[]{:S(2)}) async-start(f32[16,64,256]{2,1,0:T(8,128)} %bitcast.438), calls=%async_computation.1 | async-start | bytes 2097152 | tf_op jit(solution)/shard_map/all_to_all | solution.py:53
  140.9 47.8 %copy-start.14 = (s32[320]{0:T(512)}, s32[320]{0:T(512)S(1)}, u32[]{:S(2)}) copy-start(s32[320]{0:T(512)S(1)} %get-tuple-element.699) | copy-start | bytes 3844
  140.9 83.3 %copy-start.15 = (s32[320]{0:T(512)}, s32[320]{0:T(512)S(1)}, u32[]{:S(2)}) copy-start(s32[320]{0:T(512)S(1)} %get-tuple-element.698) | copy-start | bytes 3844
  165.9 14.1 %copy-start.7 = (s32[1024]{0:T(1024)}, s32[1024]{0:T(1024)S(1)}, u32[]{:S(2)}) copy-start(s32[1024]{0:T(1024)S(1)} %pad_clamp_fusion.12) | copy-start | bytes 12292
  165.9 46.0 %copy-start.10 = (pred[320]{0:T(512)(128)(4,1)}, pred[320]{0:T(512)(128)(4,1)S(1)}, u32[]{:S(2)}) copy-start(pred[320]{0:T(512)(128)(4,1)S(1)} %compare_reduce_fusion) | copy-start | bytes 964
  184.4 9.3 %all-to-all-start.3 = ((f32[8,8,320]{2,1,0:T(8,128)}), f32[8,8,320]{2,1,0:T(8,128)S(1)}, u32[]{:S(2)}, u32[]{:S(2)}) async-start(f32[8,8,320]{2,1,0:T(8,128)} %maximum_bitcast_fusion), calls=%async_computation.3 | async-start | bytes 196608 | tf_op jit(solution)/shard_map/all_to_all | solution.py:53
  188.7 35.6 %copy-start.13 = (s32[1024]{0:T(1024)}, s32[1024]{0:T(1024)S(1)}, u32[]{:S(2)}) copy-start(s32[1024]{0:T(1024)S(1)} %pad_clamp_fusion.11) | copy-start | bytes 12292
  224.2 21.9 %copy-start.20 = (u32[128]{0:T(128)S(1)}, u32[128]{0:T(128)}, u32[]{:S(2)}) copy-start(u32[128]{0:T(128)} %constant.350) | copy-start | bytes 1540
  227.7 12.9 %all-to-all-start.5 = ((f32[16,1,512]{2,1,0:T(1,128)}), f32[16,1,512]{2,1,0:T(1,128)S(1)}, u32[]{:S(2)}, u32[]{:S(2)}) async-start(f32[16,1,512]{2,1,0:T(1,128)} %reshape.988), calls=%async_computation.5 | async-start | bytes 65536 | tf_op jit(solution)/shard_map/all_to_all | solution.py:53
  241.7 19.7 %all-to-all-start.4 = ((f32[16,64,256]{2,1,0:T(8,128)}), f32[16,64,256]{2,1,0:T(8,128)}, u32[]{:S(2)}, u32[]{:S(2)}) async-start(f32[16,64,256]{2,1,0:T(8,128)} %broadcast_in_dim.208), calls=%async_computation.4 | async-start | bytes 2097152 | tf_op jit(solution)/shard_map/all_to_all | solution.py:23
  246.1 15.4 %copy-start.4 = (s32[1152]{0:T(1024)S(1)}, s32[1152]{0:T(1024)}, u32[]{:S(2)}) copy-start(s32[1152]{0:T(1024)} %copy-done.3) | copy-start | bytes 13828
  261.5 46.5 %copy-start.19 = (u32[128]{0:T(128)S(1)}, u32[128]{0:T(128)}, u32[]{:S(2)}) copy-start(u32[128]{0:T(128)} %constant.355) | copy-start | bytes 1540
  261.5 69.2 %copy-start.18 = (u32[128]{0:T(128)S(1)}, u32[128]{0:T(128)}, u32[]{:S(2)}) copy-start(u32[128]{0:T(128)} %constant.360) | copy-start | bytes 1540
  261.5 91.1 %copy-start.17 = (u32[128]{0:T(128)S(1)}, u32[128]{0:T(128)}, u32[]{:S(2)}) copy-start(u32[128]{0:T(128)} %constant.365) | copy-start | bytes 1540
  374.9 50.3 %all-to-all-start.7 = ((f32[16,1,512]{2,1,0:T(1,128)}), f32[16,1,512]{2,1,0:T(1,128)S(1)}, u32[]{:S(2)}, u32[]{:S(2)}) async-start(f32[16,1,512]{2,1,0:T(1,128)} %reshape.990), calls=%async_computation.7 | async-start | bytes 65536 | tf_op jit(solution)/shard_map/all_to_all | solution.py:23
  425.2 42.5 %copy-start.5 = (s32[1152]{0:T(1024)}, s32[1152]{0:T(1024)S(1)}, u32[]{:S(2)}) copy-start(s32[1152]{0:T(1024)S(1)} %get-tuple-element.1532) | copy-start | bytes 13828
  425.2 29.8 %copy-start.8 = (s32[1024]{0:T(1024)S(1)}, s32[1024]{0:T(1024)}, u32[]{:S(2)}) copy-start(s32[1024]{0:T(1024)} %copy-done.7) | copy-start | bytes 12292
  425.2 30.9 %copy-start.11 = (pred[320]{0:T(512)(128)(4,1)S(1)}, pred[320]{0:T(512)(128)(4,1)}, u32[]{:S(2)}) copy-start(pred[320]{0:T(512)(128)(4,1)} %copy-done.10) | copy-start | bytes 964
  425.3 45.1 %all-to-all-start.6 = ((f32[16,64,256]{2,1,0:T(8,128)}), f32[16,64,256]{2,1,0:T(8,128)}, u32[]{:S(2)}, u32[]{:S(2)}) async-start(f32[16,64,256]{2,1,0:T(8,128)} %bitcast.439), calls=%async_computation.6 | async-start | bytes 2097152 | tf_op jit(solution)/shard_map/all_to_all | solution.py:53
  557.9 9.9 %all-to-all-start.10 = ((f32[16,1,512]{2,1,0:T(1,128)}), f32[16,1,512]{2,1,0:T(1,128)S(1)}, u32[]{:S(2)}, u32[]{:S(2)}) async-start(f32[16,1,512]{2,1,0:T(1,128)} %reshape.992), calls=%async_computation.10 | async-start | bytes 65536 | tf_op jit(solution)/shard_map/all_to_all | solution.py:53
  568.8 19.8 %all-to-all-start.9 = ((f32[16,64,256]{2,1,0:T(8,128)}), f32[16,64,256]{2,1,0:T(8,128)}, u32[]{:S(2)}, u32[]{:S(2)}) async-start(f32[16,64,256]{2,1,0:T(8,128)} %broadcast_in_dim.210), calls=%async_computation.9 | async-start | bytes 2097152 | tf_op jit(solution)/shard_map/all_to_all | solution.py:23
  573.2 15.5 %copy-start.6 = (s32[1152]{0:T(1024)S(1)}, s32[1152]{0:T(1024)}, u32[]{:S(2)}) copy-start(s32[1152]{0:T(1024)} %copy-done.5) | copy-start | bytes 13828
  713.0 50.3 %all-to-all-start.12 = ((f32[16,1,512]{2,1,0:T(1,128)}), f32[16,1,512]{2,1,0:T(1,128)S(1)}, u32[]{:S(2)}, u32[]{:S(2)}) async-start(f32[16,1,512]{2,1,0:T(1,128)} %reshape.994), calls=%async_computation.12 | async-start | bytes 65536 | tf_op jit(solution)/shard_map/all_to_all | solution.py:23
  763.3 48.4 %copy-start.2 = (f32[8,1536]{1,0:T(8,128)}, f32[8,1536]{1,0:T(8,128)S(1)}, u32[]{:S(2)}) copy-start(f32[8,1536]{1,0:T(8,128)S(1)} %get-tuple-element.1496) | copy-start | bytes 147460
  763.3 35.6 %copy-start.9 = (s32[1024]{0:T(1024)S(1)}, s32[1024]{0:T(1024)}, u32[]{:S(2)}) copy-start(s32[1024]{0:T(1024)} %copy-done.7) | copy-start | bytes 12292
  763.3 36.7 %copy-start.12 = (pred[320]{0:T(512)(128)(4,1)S(1)}, pred[320]{0:T(512)(128)(4,1)}, u32[]{:S(2)}) copy-start(pred[320]{0:T(512)(128)(4,1)} %copy-done.10) | copy-start | bytes 964
  763.3 51.0 %all-to-all-start.11 = ((f32[16,64,256]{2,1,0:T(8,128)}), f32[16,64,256]{2,1,0:T(8,128)}, u32[]{:S(2)}, u32[]{:S(2)}) async-start(f32[16,64,256]{2,1,0:T(8,128)} %bitcast.440), calls=%async_computation.11 | async-start | bytes 2097152 | tf_op jit(solution)/shard_map/all_to_all | solution.py:53
  816.2 10.6 %all-to-all-start.13 = ((f32[8,8,320]{2,1,0:T(8,128)}), f32[8,8,320]{2,1,0:T(8,128)S(1)}, u32[]{:S(2)}, u32[]{:S(2)}) async-start(f32[8,8,320]{2,1,0:T(8,128)} %maximum_bitcast_fusion.2), calls=%async_computation.13 | async-start | bytes 196608 | tf_op jit(solution)/shard_map/all_to_all | solution.py:53
Sparse Core Ops, SparseCore 0:
  10.2 50.6 all-gather.1
